TPU v7x, 32 devices: a whole 2x2x4 slice. The times are simulated.
32 devices in a mesh: groups: 2 (over y), cand: 4 (over z), mp: 4 (over x, core).
Axes of the slice: x: 2, y: 2, z: 4, core: 2. Of those that a mesh axis runs over, the one named last changes fastest.
Arguments:
- user_feats: bfloat16 [8, 4096], P(('groups', 'cand')), parts along dimension 0, may hold values from -6 to 6
- user_slot: int32 [2], P('groups'), parts along dimension 0, may hold values from 0 to 3, as said below
- cand_pool: bfloat16 [512, 4096], P('groups'), parts along dimension 0, may hold values from -6 to 6
- cand_ids: int32 [2, 64], P('groups'), parts along dimension 0, may hold values from 0 to 255
- first_weight: bfloat16 [8192, 8192], P('mp', 'cand'), may hold values from -0.0625 to 0.0625
- first_bias: float32 [8192], P('cand'), may hold values from -5 to 5
- second_weight: bfloat16 [8192, 8192], P('cand', 'mp'), may hold values from -0.0625 to 0.0625
- second_bias: float32 [8192], P('mp'), may hold values from -5 to 5
- third_weight: bfloat16 [8192, 8192], P('mp', 'cand'), may hold values from -0.0625 to 0.0625
- third_bias: float32 [8192], P('cand'), may hold values from -5 to 5
- score_weight: bfloat16 [8192], P('cand'), may hold values from -0.0625 to 0.0625
Outputs:
- crossed: bfloat16 [128, 8192], P(('groups', 'mp'), 'cand'), parts along dimension 0
- logits: float32 [128], P(('groups', 'mp')), parts along dimension 0
There are 2 independent parts, one for each index of `groups`. A program takes and returns all parts, laid end to end along the dimension named above; an argument that names none is the same for every part. Nothing has to cross between parts.
Inputs may be any that keep to these rules, and one draw needn't show every extreme that they name: `user_slot`: the users' slots are distinct.
All inputs are finite; a program needn't handle non-finite values.
Results may differ from a plain program's by a relative error of at most 0.022.
Values may be sent and summed in bfloat16 or wider, within the bound.
A program may use at most 64 MiB of HBM per device.

v0:
```python
import jax
import jax.numpy as jnp
from jax import lax
from jax.experimental import pallas as pl
from jax.experimental.pallas import tpu as pltpu
from jax.sharding import PartitionSpec as P

MESH = pl.DeviceIdType.MESH
F32 = jnp.float32
BF16 = jnp.bfloat16


def reverse_bits(value, bits):
    out = 0
    for _ in range(bits):
        out = 2 * out + value % 2
        value //= 2
    return out


def hand_on(crossed_ref, logit_ref, crossed_hbm, logit_hbm, sem):
    copies = [
        pltpu.make_async_copy(crossed_ref, crossed_hbm, sem.at[0]),
        pltpu.make_async_copy(logit_ref, logit_hbm, sem.at[1]),
    ]
    for copy in copies:
        copy.start()
    for copy in copies:
        copy.wait()


def make_kernel(n_mp, n_cand, shapes):
    rows, per_user, users, slots_each, half_width, pool_count, feat, col, n1, n2 = shapes
    cw1, cw2 = col // n1, feat // n2
    bits = n_mp.bit_length() - 1
    block = rows // n_mp
    ratio = feat // col
    group = n_mp * n_cand

    def kernel(
        user_hbm, slot_ref, pool_hbm, ids_hbm, w1_hbm, b1_hbm, w2_hbm, b2_hbm, w3_hbm, b3_hbm, score_hbm,
        out_ref, logit_ref,
        user_ref, ids_ref, b1_ref, b2_ref, b3_ref, score_ref, small_sem, slots, pool_v, w1_v, w2_v, w3_v, onehot, base_mp, base_col,
        acc1, send1, recv1, cross1, acc2, q_send, l_recv, r_recv, l_send, r_send, x3, acc3, send3, recv3, q_rows, q_all,
        w_sem, user_ss, user_rs, a_ss, a_rs, g_ss, g_rs, l_ss, l_rs, r_ss, r_rs, c_ss, c_rs, q_ss, q_rs,
    ):
        i = lax.axis_index("mp")
        j = lax.axis_index("cand")
        me = i * n_cand + j
        pending = []

        def remote(src, dst, ss, rs, where):
            return pltpu.make_async_remote_copy(
                src_ref=src, dst_ref=dst, send_sem=ss, recv_sem=rs, device_id=where, device_id_type=MESH
            )

        small_copies = [
            pltpu.make_async_copy(src, dst, small_sem.at[k])
            for k, (src, dst) in enumerate(
                (
                    (user_hbm, user_ref), (ids_hbm, ids_ref), (b1_hbm, b1_ref),
                    (b2_hbm, b2_ref), (b3_hbm, b3_ref), (score_hbm, score_ref),
                )
            )
        ]
        for copy in small_copies:
            copy.start()
        barrier = pltpu.get_barrier_semaphore()

        def greet(d, carry):
            peer = lax.rem(me + d, group)
            pl.semaphore_signal(
                barrier, inc=1, device_id={"mp": peer // n_cand, "cand": lax.rem(peer, n_cand)}, device_id_type=MESH
            )
            return carry

        lax.fori_loop(1, group, greet, 0)

        pool_copy = pltpu.make_async_copy(pool_hbm, pool_v, w_sem.at[0])
        w1_copies = [
            pltpu.make_async_copy(w1_hbm.at[:, pl.ds(c * cw1, cw1)], w1_v.at[c], w_sem.at[1 + c]) for c in range(n1)
        ]
        w2_copies = [
            pltpu.make_async_copy(w2_hbm.at[pl.ds(c * cw1, cw1), :], w2_v.at[pl.ds(c * cw1, cw1), :], w_sem.at[1 + n1 + c])
            for c in range(n1)
        ]
        w3_copies = [
            pltpu.make_async_copy(w3_hbm.at[pl.ds(c * cw2, cw2), :], w3_v.at[pl.ds(c * cw2, cw2), :], w_sem.at[1 + 2 * n1 + c])
            for c in range(n2)
        ]
        pool_copy.start()
        for copy in w1_copies:
            copy.start()

        small_copies[0].wait()
        pl.semaphore_wait(barrier, group - 1)

        def user_copy(d):
            return remote(
                user_ref, slots.at[j], user_ss.at[d - 1], user_rs.at[j], {"cand": lax.rem(j + d, n_cand)}
            )

        for d in range(1, n_cand):
            user_copy(d).start()
        slots[j] = user_ref[...]
        small_copies[1].wait()

        for u in range(users):
            hot = (
                lax.broadcasted_iota(jnp.int32, (pool_count, per_user), 0) == ids_ref[u : u + 1, :]
            ).astype(F32).T
            for p in range(n_mp):
                first = reverse_bits(p, bits) * block
                if first // per_user == u:
                    off = first % per_user
                    onehot[p * block : (p + 1) * block, :] = hot[off : off + block].astype(BF16)

        def from_pool(dst, index, width):
            @pl.when(index >= half_width // width)
            def _():
                for c in range(0, width, 256):
                    start = pl.multiple_of(index * width - half_width + c, 128)
                    dst[:, c : c + 256] = jnp.dot(
                        onehot[...], pool_v[:, pl.ds(start, 256)], preferred_element_type=F32
                    ).astype(BF16)

        def from_user(dst, index, width):
            @pl.when(index < half_width // width)
            def _():
                start = pl.multiple_of(index * width, 128)
                for p in range(n_mp):
                    slot = slot_ref[(reverse_bits(p, bits) * block) // per_user]
                    row = slots[slot // slots_each, :, pl.ds(start, width)].astype(F32)
                    if slots_each > 1:
                        pick = lax.broadcasted_iota(jnp.int32, row.shape, 0) == lax.rem(slot, slots_each)
                        row = jnp.sum(jnp.where(pick, row, 0.0), axis=0, keepdims=True)
                    dst[p * block : (p + 1) * block, :] = jnp.broadcast_to(row, (block, width)).astype(BF16)

        def from_all_users():
            for d in range(1, n_cand):
                k = lax.rem(j - d + n_cand, n_cand)
                remote(user_ref, slots.at[k], user_ss.at[d - 1], user_rs.at[k], {"cand": k}).wait_recv()

        pool_copy.wait()
        from_pool(base_mp, i, feat)
        user_side = i < half_width // feat

        @pl.when(user_side)
        def _():
            from_pool(base_col, j, col)
            from_all_users()
            from_user(base_mp, i, feat)

        def bit_of(b):
            return lax.rem(i // (1 << b), 2)

        def partner(b):
            return i + (1 << b) * (1 - 2 * bit_of(b))

        lows = [0]
        for b in range(bits):
            lows.append(lows[b] + bit_of(b) * (rows >> (b + 1)))

        def seg(b):
            size = rows >> b
            if b == 0:
                return pl.ds(0, rows)
            return pl.ds(pl.multiple_of(lows[b], size), size)

        def other(b):
            size = rows >> (b + 1)
            low = lows[b] + (1 - bit_of(b)) * size
            return pl.ds(pl.multiple_of(low, size), size)

        last = bits - 1

        def scatter_copy(c, b):
            rng = other(b) if b < last else seg(b)
            size = rows >> min(b + 1, last)
            return remote(
                send1.at[c, rng, :], recv1.at[b, c, pl.ds(0, size), :], a_ss.at[b, c], a_rs.at[b, c], {"mp": partner(b)}
            )

        def gather_copy(c, b):
            return remote(
                cross1.at[c, seg(b + 1), :], cross1.at[c, seg(b + 1), :], g_ss.at[b, c], g_rs.at[b, c], {"mp": partner(b)}
            )

        def gather_wait(c, b):
            remote(
                cross1.at[c, other(b), :], cross1.at[c, other(b), :], g_ss.at[b, c], g_rs.at[b, c], {"mp": partner(b)}
            ).wait_recv()

        def stage_a(c):
            w1_copies[c].wait()
            term = jnp.dot(base_mp[...], w1_v[c], preferred_element_type=F32)
            acc1[c] = term
            send1[c] = term.astype(BF16)
            copy = scatter_copy(c, 0)
            copy.start()
            pending.append(copy)

        def stage_b(c):
            for b in range(last):
                scatter_copy(c, b).wait_recv()
                size = rows >> (b + 1)
                term = acc1[c, seg(b + 1), :] + recv1[b, c, 0:size, :].astype(F32)
                if b + 1 < last:
                    acc1[c, seg(b + 1), :] = term
                send1[c, seg(b + 1), :] = term.astype(BF16)
                copy = scatter_copy(c, b + 1)
                copy.start()
                pending.append(copy)

        def stage_c(c):
            scatter_copy(c, last).wait_recv()
            size = rows >> last
            total = send1[c, seg(last), :].astype(F32) + recv1[last, c, 0:size, :].astype(F32)
            cols = slice(c * cw1, (c + 1) * cw1)
            base = base_col[seg(last), cols].astype(F32)
            cross1[c, seg(last), :] = (base * (total + b1_ref[:, cols]) + base).astype(BF16)
            if last > 0:
                copy = gather_copy(c, last - 1)
                copy.start()
                pending.append(copy)

        def line_copy(n, right, first):
            src = (q_send if first else (l_send if right else r_send)).at[n]
            if right:
                return remote(src, l_recv.at[n], l_ss.at[n], l_rs.at[n], {"cand": j + 1})
            return remote(src, r_recv.at[n], r_ss.at[n], r_rs.at[n], {"cand": j - 1})

        def stage_d(c):
            for b in range(last - 1, -1, -1):
                gather_wait(c, b)
                if b > 0:
                    copy = gather_copy(c, b - 1)
                    copy.start()
                    pending.append(copy)
            w2_copies[c].wait()
            for n in range(n2):
                cols = slice(n * cw2, (n + 1) * cw2)
                term = jnp.dot(
                    cross1[c], w2_v[c * cw1 : (c + 1) * cw1, cols], preferred_element_type=F32
                )
                if c > 0:
                    term = acc2[:, cols] + term
                if c < n1 - 1:
                    acc2[:, cols] = term
                    continue
                owner = (j == i * ratio + (n * cw2) // col).astype(F32)
                inner = (n * cw2) % col
                carried = cross1[inner // cw1, :, inner % cw1 : inner % cw1 + cw2].astype(F32)
                term = base_mp[:, cols].astype(F32) * (term + owner * b2_ref[:, cols]) + owner * carried
                q_send[n] = term.astype(BF16)

                @pl.when(j == 0)
                def _():
                    line_copy(n, True, True).start()

                @pl.when(j == n_cand - 1)
                def _():
                    line_copy(n, False, True).start()

        order = []
        for s in range(n1 + 1):
            if s < n1:
                order.append((stage_a, s))
            if s >= 1:
                order.append((stage_b, s - 1))
        for s in range(n1 + 1):
            if s < n1:
                order.append((stage_c, s))
            if s >= 1:
                order.append((stage_d, s - 1))
        started = False
        for stage, c in order:
            if stage is stage_c and c == 0:
                @pl.when(jnp.logical_not(user_side))
                def _():
                    from_pool(base_col, j, col)
                    from_all_users()

                from_user(base_col, j, col)
                for copy in small_copies[2:]:
                    copy.wait()
            stage(c)
            if stage is stage_a and c == n1 - 1:
                for copy in w2_copies:
                    copy.start()
            if stage is stage_c and not started:
                started = True
                for copy in w3_copies:
                    copy.start()

        def forward(n, right):
            came = (l_recv if right else r_recv)[n].astype(F32)
            (l_send if right else r_send)[n] = (came + q_send[n].astype(F32)).astype(BF16)
            line_copy(n, right, False).start()

        def take(n, right):
            if right:
                remote(l_send.at[n], l_recv.at[n], l_ss.at[n], l_rs.at[n], {"cand": j}).wait_recv()
            else:
                remote(r_send.at[n], r_recv.at[n], r_ss.at[n], r_rs.at[n], {"cand": j}).wait_recv()

        def third(n):
            w3_copies[n].wait()
            for p in range(n1):
                cols = slice(p * cw1, (p + 1) * cw1)
                term = jnp.dot(
                    x3[:, n * cw2 : (n + 1) * cw2], w3_v[n * cw2 : (n + 1) * cw2, cols], preferred_element_type=F32
                )
                if n > 0:
                    term = acc3[:, cols] + term
                acc3[:, cols] = term

        skew = min(3, n2)
        near_left = j < (n_cand + 1) // 2
        inner_device = jnp.logical_and(j > 0, j < n_cand - 1)
        for s in range(n2 + skew):
            if s < n2:
                @pl.when(jnp.logical_and(inner_device, near_left))
                def _():
                    take(s, True)
                    forward(s, True)

                @pl.when(jnp.logical_and(inner_device, jnp.logical_not(near_left)))
                def _():
                    take(s, False)
                    forward(s, False)

            n = s - skew
            if n < 0:
                continue

            @pl.when(jnp.logical_and(inner_device, near_left))
            def _():
                take(n, False)
                forward(n, False)

            @pl.when(jnp.logical_and(inner_device, jnp.logical_not(near_left)))
            def _():
                take(n, True)
                forward(n, True)

            cols = slice(n * cw2, (n + 1) * cw2)

            @pl.when(inner_device)
            def _():
                x3[:, cols] = (
                    q_send[n].astype(F32) + l_recv[n].astype(F32) + r_recv[n].astype(F32)
                ).astype(BF16)

            @pl.when(j == 0)
            def _():
                take(n, False)
                x3[:, cols] = (q_send[n].astype(F32) + r_recv[n].astype(F32)).astype(BF16)

            @pl.when(j == n_cand - 1)
            def _():
                take(n, True)
                x3[:, cols] = (q_send[n].astype(F32) + l_recv[n].astype(F32)).astype(BF16)

            third(n)

        def last_copy(c, b):
            size = rows >> (b + 1)
            return remote(
                send3.at[c, other(b), :], recv3.at[b, c, pl.ds(0, size), :], c_ss.at[b, c], c_rs.at[b, c], {"mp": partner(b)}
            )

        owner = (i == j // ratio).astype(F32)
        lanes = jnp.zeros((rows, 128), F32)
        for c in range(n1):
            cols = slice(c * cw1, (c + 1) * cw1)
            if ratio == 1:
                carried = x3[:, cols]
            else:
                carried = x3[:, pl.ds(pl.multiple_of(lax.rem(j, ratio) * col + c * cw1, 128), cw1)]
            term = (
                base_col[:, cols].astype(F32) * (acc3[:, cols] + owner * b3_ref[:, cols])
                + owner * carried.astype(F32)
            )
            acc3[:, cols] = term
            send3[c] = term.astype(BF16)
            copy = last_copy(c, 0)
            copy.start()
            pending.append(copy)
            scored = term * score_ref[cols].astype(F32).reshape(1, cw1)
            for k in range(0, cw1, 128):
                lanes = lanes + scored[:, k : k + 128]
        q_rows[...] = jnp.zeros_like(q_rows)
        q_rows[0:rows, :] = lanes
        q_all[me] = jnp.sum(q_rows[...].T, axis=0, keepdims=True)

        def q_copy(d):
            peer = lax.rem(me + d, group)
            return remote(
                q_all.at[me], q_all.at[me], q_ss.at[d], q_rs.at[me],
                {"mp": peer // n_cand, "cand": lax.rem(peer, n_cand)},
            )

        def q_start(d, carry):
            q_copy(d).start()
            return carry

        lax.fori_loop(1, group, q_start, 0)

        for b in range(bits):
            for c in range(n1):
                cols = slice(c * cw1, (c + 1) * cw1)
                last_copy(c, b).wait_recv()
                size = rows >> (b + 1)
                term = acc3[seg(b + 1), cols] + recv3[b, c, 0:size, :].astype(F32)
                if b + 1 < bits:
                    acc3[seg(b + 1), cols] = term
                    send3[c, seg(b + 1), :] = term.astype(BF16)
                    copy = last_copy(c, b + 1)
                    copy.start()
                    pending.append(copy)
                else:
                    out_ref[:, cols] = term.astype(BF16)

        def q_wait(d, carry):
            k = lax.rem(me - d + group, group)
            remote(q_all.at[k], q_all.at[k], q_ss.at[d], q_rs.at[k], {"cand": j}).wait_recv()
            return carry

        lax.fori_loop(1, group, q_wait, 0)
        total = jnp.sum(q_all[...], axis=0)
        for k in range(n_mp):
            p = reverse_bits(k, bits)

            @pl.when(i == k)
            def _():
                logit_ref[...] = total[:, p * block : (p + 1) * block]

        for copy in pending:
            copy.wait_send()
        for d in range(1, n_cand):
            user_copy(d).wait_send()

        def q_sent(d, carry):
            q_copy(d).wait_send()
            return carry

        lax.fori_loop(1, group, q_sent, 0)
        for n in range(n2):
            @pl.when(j < n_cand - 1)
            def _():
                line_copy(n, True, False).wait_send()

            @pl.when(j > 0)
            def _():
                line_copy(n, False, False).wait_send()

    return kernel


def solution(mesh):
    n_mp, n_cand = mesh.shape["mp"], mesh.shape["cand"]

    def body(
        user_feats, user_slot, cand_pool, cand_ids, first_weight, first_bias,
        second_weight, second_bias, third_weight, third_bias, score_weight,
    ):
        slots_each, half_width = user_feats.shape
        users, per_user = cand_ids.shape
        rows = users * per_user
        pool_count = cand_pool.shape[0]
        feat, col = first_weight.shape
        n1 = max(1, col // 512)
        n2 = max(1, feat // 256)
        cw1, cw2 = col // n1, feat // n2
        bits = n_mp.bit_length() - 1
        block = rows // n_mp
        group = n_mp * n_cand
        shapes = (rows, per_user, users, slots_each, half_width, pool_count, feat, col, n1, n2)
        vmem = pl.BlockSpec(memory_space=pltpu.VMEM)
        smem = pl.BlockSpec(memory_space=pltpu.SMEM)
        hbm = pl.BlockSpec(memory_space=pl.ANY)
        dma = pltpu.SemaphoreType.DMA
        exchange = rows >> (1 if bits > 1 else 0)
        crossed, logits = pl.pallas_call(
            make_kernel(n_mp, n_cand, shapes),
            out_shape=(
                pltpu.VMEM((block, col), BF16),
                pltpu.VMEM((1, block), F32),
            ),
            in_specs=[hbm, smem] + [hbm] * 9,
            out_specs=(vmem, vmem),
            scratch_shapes=[
                pltpu.VMEM((slots_each, half_width), BF16),
                pltpu.VMEM((users, per_user), jnp.int32),
                pltpu.VMEM((1, col), F32),
                pltpu.VMEM((1, feat), F32),
                pltpu.VMEM((1, col), F32),
                pltpu.VMEM((col,), BF16),
                dma((6,)),
                pltpu.VMEM((n_cand, slots_each, half_width), BF16),
                pltpu.VMEM((pool_count, half_width), BF16),
                pltpu.VMEM((n1, feat, cw1), BF16),
                pltpu.VMEM((col, feat), BF16),
                pltpu.VMEM((feat, col), BF16),
                pltpu.VMEM((rows, pool_count), BF16),
                pltpu.VMEM((rows, feat), BF16),
                pltpu.VMEM((rows, col), BF16),
                pltpu.VMEM((n1, rows, cw1), F32),
                pltpu.VMEM((n1, rows, cw1), BF16),
                pltpu.VMEM((bits, n1, exchange, cw1), BF16),
                pltpu.VMEM((n1, rows, cw1), BF16),
                pltpu.VMEM((rows, feat), F32),
                pltpu.VMEM((n2, rows, cw2), BF16),
                pltpu.VMEM((n2, rows, cw2), BF16),
                pltpu.VMEM((n2, rows, cw2), BF16),
                pltpu.VMEM((n2, rows, cw2), BF16),
                pltpu.VMEM((n2, rows, cw2), BF16),
                pltpu.VMEM((rows, feat), BF16),
                pltpu.VMEM((rows, col), F32),
                pltpu.VMEM((n1, rows, cw1), BF16),
                pltpu.VMEM((bits, n1, rows // 2, cw1), BF16),
                pltpu.VMEM((max(rows, 128), 128), F32),
                pltpu.VMEM((group, 1, max(rows, 128)), F32),
                dma((1 + 2 * n1 + n2,)),
                dma((n_cand,)),
                dma((n_cand,)),
                dma((bits, n1)),
                dma((bits, n1)),
                dma((bits, n1)),
                dma((bits, n1)),
                dma((n2,)),
                dma((n2,)),
                dma((n2,)),
                dma((n2,)),
                dma((bits, n1)),
                dma((bits, n1)),
                dma((group,)),
                dma((group,)),
            ],
            compiler_params=pltpu.CompilerParams(
                collective_id=0, has_side_effects=True, vmem_limit_bytes=67043328 - 3000 * 1024
            ),
        )(
            user_feats, user_slot, cand_pool, cand_ids, first_weight, first_bias.reshape(1, -1),
            second_weight, second_bias.reshape(1, -1), third_weight, third_bias.reshape(1, -1),
            score_weight,
        )
        crossed, logits = pl.pallas_call(
            hand_on,
            out_shape=(
                jax.ShapeDtypeStruct((block, col), BF16),
                jax.ShapeDtypeStruct((1, block), F32),
            ),
            in_specs=[vmem, vmem],
            out_specs=(hbm, hbm),
            scratch_shapes=[dma((2,))],
            compiler_params=pltpu.CompilerParams(vmem_limit_bytes=1024 * 1024),
        )(crossed, logits)
        return crossed, logits.reshape(-1)

    in_specs = (
        P(("groups", "cand"), None),
        P("groups"),
        P("groups", None),
        P("groups", None),
        P("mp", "cand"),
        P("cand"),
        P("cand", "mp"),
        P("mp"),
        P("mp", "cand"),
        P("cand"),
        P("cand"),
    )
    out_specs = (P(("groups", "mp"), "cand"), P(("groups", "mp")))
    return jax.shard_map(body, mesh=mesh, in_specs=in_specs, out_specs=out_specs, check_vma=False)
```

profile of v0, /device:TPU:0, one launch (start us, length us, event | category | flops | bytes accessed | tf_op | source)
XLA Modules:
  0.0 40.1 jit_solution(7856664079961805269)
XLA Ops:
  1.3 38.1 %shard_map.122 = (bf16[16,2048]{1,0:T(8,128)(2,1)S(1)}, f32[1,16]{1,0:T(1,128)S(1)}) custom-call(bf16[1,4096]{1,0:T(2,128)(2,1)} %user_hbm.1, s32[1]{0:T(128)S(6)} %copy.13.slot_ref, bf16[256,4096]{1,0:T(8,128)(2,1)} %pool_hbm.1, s32[1,64]{1,0:T(1,128)} %ids_hbm.1, bf16[2048,2048]{1,0:T(8,128)(2,1)} %w1_hbm.1, f32[1,2048]{1,0:T(1,128)} %bitcast.4, ...), custom_call_target="tpu_custom_call" | custom-call | tf_op jit(solution)/shard_map/pallas_call | solution.py:485
  39.4 0.7 %shard_map.123 = (bf16[16,2048]{1,0:T(8,128)(2,1)}, f32[1,16]{1,0:T(1,128)}) custom-call(bf16[16,2048]{1,0:T(8,128)(2,1)S(1)} %get-tuple-element.6.crossed_ref, f32[1,16]{1,0:T(1,128)S(1)} %get-tuple-element.7.logit_ref), custom_call_target="tpu_custom_call" | custom-call | tf_op jit(solution)/shard_map/pallas_call | solution.py:549
where the time goes:
time: 40.3 us; the launch traced here: 40.1 us
  Pallas kernels  38.8 us (96%)
  between operations  1.29 us (3%)
    pallas_call x1, Pallas kernels, body(): pl.pallas_call(make_kernel(n_mp, n_cand, shapes), out_shape=(pltpu.VMEM((...  38.1 us

commit v1 on v0

--- a/solution.py
+++ b/solution.py
@@ -315,7 +315,7 @@
                     term = acc3[:, cols] + term
                 acc3[:, cols] = term
 
-        skew = min(3, n2)
+        skew = min(4, n2)
         near_left = j < (n_cand + 1) // 2
         inner_device = jnp.logical_and(j > 0, j < n_cand - 1)
         for s in range(n2 + skew):

time: 40.3 us -> 40 us (level)
  no operation moved by 1% of the time
where the time goes in v1:
time: 40 us; the launch traced here: 39.7 us
  Pallas kernels  38.4 us (96%)
  between operations  1.29 us (3%)
    pallas_call x1, Pallas kernels, body(): pl.pallas_call(make_kernel(n_mp, n_cand, shapes), out_shape=(pltpu.VMEM((...  37.8 us

profile of v1, /device:TPU:0, one launch (start us, length us, event | category | flops | bytes accessed | tf_op | source)
XLA Modules:
  0.0 39.7 jit_solution(11286547125417754144)
XLA Ops:
  1.3 37.8 %shard_map.122 = (bf16[16,2048]{1,0:T(8,128)(2,1)S(1)}, f32[1,16]{1,0:T(1,128)S(1)}) custom-call(bf16[1,4096]{1,0:T(2,128)(2,1)} %user_hbm.1, s32[1]{0:T(128)S(6)} %copy.13.slot_ref, bf16[256,4096]{1,0:T(8,128)(2,1)} %pool_hbm.1, s32[1,64]{1,0:T(1,128)} %ids_hbm.1, bf16[2048,2048]{1,0:T(8,128)(2,1)} %w1_hbm.1, f32[1,2048]{1,0:T(1,128)} %bitcast.4, ...), custom_call_target="tpu_custom_call" | custom-call | tf_op jit(solution)/shard_map/pallas_call | solution.py:485
  39.0 0.7 %shard_map.123 = (bf16[16,2048]{1,0:T(8,128)(2,1)}, f32[1,16]{1,0:T(1,128)}) custom-call(bf16[16,2048]{1,0:T(8,128)(2,1)S(1)} %get-tuple-element.6.crossed_ref, f32[1,16]{1,0:T(1,128)S(1)} %get-tuple-element.7.logit_ref), custom_call_target="tpu_custom_call" | custom-call | tf_op jit(solution)/shard_map/pallas_call | solution.py:549
